TPU v7x, 32 devices: a whole 2x2x4 slice. The times are simulated.
32 devices in a mesh: unit: 2 (over y), row: 4 (over x, core), col: 4 (over z).
Axes of the slice: x: 2, y: 2, z: 4, core: 2. Of those that a mesh axis runs over, the one named last changes fastest.
Arguments:
- tracer: float32 [4, 32, 64, 64], P('unit', None, 'row', 'col'), parts along dimension 0, may hold values from -6 to 6
- symbol_x: float32 [32], replicated, may hold values from 0.3 to 3
- symbol_y: float32 [64], replicated, may hold values from 0.3 to 3
- symbol_z: float32 [64], replicated, may hold values from 0.3 to 3
Outputs:
- smoothed: float32 [4, 32, 64, 64], P('unit', None, 'row', 'col'), parts along dimension 0
There are 2 independent parts, one for each index of `unit`. A program takes and returns all parts, laid end to end along the dimension named above; an argument that names none is the same for every part. Nothing has to cross between parts.
All inputs are finite; a program needn't handle non-finite values.
Results may differ from a plain program's by a relative error of at most 0.0003.
Values sent between devices are 32-bit elements.
A program may use at most 64 MiB of HBM per device.

v0:
```python
import jax
import jax.numpy as jnp
from jax import lax
from jax.sharding import PartitionSpec as P


def mode_table(count):
    rank = jnp.arange(count)
    angle = (
        jnp.pi
        / (4 * count)
        * ((2 * rank[:, None] + 1) * (2 * rank[None, :] + 1) % (8 * count)).astype(jnp.float32)
    )
    return jnp.cos(angle) * (2.0 / count) ** 0.5


def to_modes(values, dim):
    moved = jnp.tensordot(
        values, mode_table(values.shape[dim]), axes=([dim], [0]), precision=lax.Precision.HIGHEST
    )
    return jnp.moveaxis(moved, -1, dim)


def shards(tracer, symbol_x, symbol_y, symbol_z):

    def forward_part(part_values):
        part_values = to_modes(part_values, 1)
        part_values = lax.all_to_all(part_values, "row", split_axis=1, concat_axis=2, tiled=True)
        part_values = to_modes(part_values, 2)
        part_values = lax.all_to_all(part_values, "col", split_axis=2, concat_axis=3, tiled=True)
        return to_modes(part_values, 3)

    def backward_part(part_values):
        part_values = to_modes(part_values, 3)
        part_values = lax.all_to_all(part_values, "col", split_axis=3, concat_axis=2, tiled=True)
        part_values = to_modes(part_values, 2)
        part_values = lax.all_to_all(part_values, "row", split_axis=2, concat_axis=1, tiled=True)
        return to_modes(part_values, 1)

    block_values = forward_part(tracer)
    share_x = block_values.shape[1]
    part_x = lax.dynamic_slice_in_dim(symbol_x, lax.axis_index("row") * share_x, share_x)
    share_y = block_values.shape[2]
    part_y = lax.dynamic_slice_in_dim(symbol_y, lax.axis_index("col") * share_y, share_y)
    symbol = part_x[:, None, None] + part_y[None, :, None] + symbol_z[None, None, :]
    block_values = block_values * lax.rsqrt(symbol)
    block_values = backward_part(block_values)
    return block_values


def solution(mesh):
    in_specs = (P("unit", None, "row", "col"), P(), P(), P())
    out_specs = P("unit", None, "row", "col")
    return jax.shard_map(shards, mesh=mesh, in_specs=in_specs, out_specs=out_specs, check_vma=False)
```

profile of v0, /device:TPU:0, one launch (start us, length us, event | category | flops | bytes accessed | tf_op | source)
XLA Modules:
  0.0 49.6 jit_solution(17201556135171199942)
XLA Ops:
  0.0 0.0 copy-start
  0.0 0.9 %copy-done = f32[2,32,16,16]{1,3,2,0:T(8,128)S(1)} copy-done((f32[2,32,16,16]{1,3,2,0:T(8,128)S(1)}, f32[2,32,16,16]{1,3,2,0:T(8,128)}, u32[]{:S(2)}) %copy-start) | copy-done | bytes 65560
  1.0 0.5 %fusion.47 = f32[32,512]{0,1:S(1)} fusion(f32[32,512]{0,1:T(8,128)S(1)} %bitcast.57, s32[32]{0:T(128)S(1)} %multiply_add_fusion.1), kind=kOutput, calls=%fused_computation.59 | convolution fusion | flops 6306816 | bytes 131200
  1.5 0.5 copy.14
  1.9 0.9 %reshape.67 = f32[4,1,4096]{2,1,0:T(1,128)} reshape(f32[32,2,16,16]{3,2,1,0:T(8,128)S(1)} %bitcast.61) | data formatting | bytes 131072
  2.8 4.2 %all-to-all-start = ((f32[4,1,4096]{2,1,0:T(1,128)}), f32[4,1,4096]{2,1,0:T(1,128)S(1)}, u32[]{:S(2)}, u32[]{:S(2)}) async-start(f32[4,1,4096]{2,1,0:T(1,128)} %reshape.67), calls=%async_computation | async-start | bytes 131072 | tf_op jit(solution)/shard_map/all_to_all | solution.py:28
  7.0 0.0 copy-start.2
  7.0 0.7 %copy-done.2 = f32[64]{0:T(128)S(1)} copy-done((f32[64]{0:T(128)S(1)}, f32[64]{0:T(128)}, u32[]{:S(2)}) %copy-start.2) | copy-done | bytes 280
  7.7 0.1 dynamic_slice.7
  7.8 0.0 copy-start.3
  7.8 0.7 %copy-done.3 = f32[32]{0:T(128)S(1)} copy-done((f32[32]{0:T(128)S(1)}, f32[32]{0:T(128)}, u32[]{:S(2)}) %copy-start.3) | copy-done | bytes 152
  8.4 0.1 dynamic_slice.6
  8.5 0.1 broadcast_add_fusion
  8.6 2.6 %all-to-all-done = f32[4,1,4096]{2,1,0:T(1,128)S(1)} async-done(((f32[4,1,4096]{2,1,0:T(1,128)}), f32[4,1,4096]{2,1,0:T(1,128)S(1)}, u32[]{:S(2)}, u32[]{:S(2)}) %all-to-all-start) | async-done | bytes 65568 | tf_op jit(solution)/shard_map/all_to_all | solution.py:28
  11.2 0.6 %broadcast.193 = f32[]{:T(128)} broadcast(f32[]{:T(128)} %constant.155), dimensions={} | broadcast | bytes 8 | tf_op jit(solution)/shard_map/all_to_all | solution.py:28
  11.8 0.9 %reduce = f32[4,4096]{1,0:T(4,128)S(1)} reduce(f32[4,1,4096]{2,1,0:T(1,128)S(1)} %all-to-all-done, f32[]{:T(128)} %broadcast.193), dimensions={1}, to_apply=%all_to_all.52.reduce_sub_computation | reduce | bytes 131076 | tf_op jit(solution)/shard_map/all_to_all | solution.py:28
  12.6 0.2 reshape.68
  12.8 0.2 copy.16
  13.1 0.3 all_to_all.55
  13.3 0.5 convolution_bitcast_fusion.2
  13.8 0.3 copy.17
  14.1 0.9 %reshape.69 = f32[4,1,4096]{2,1,0:T(1,128)} reshape(f32[64,2,8,16]{3,2,1,0:T(8,128)S(1)} %bitcast.58) | data formatting | bytes 131072
  14.9 0.0 copy-start.1
  14.9 5.5 %all-to-all-start.1 = ((f32[4,1,4096]{2,1,0:T(1,128)}), f32[4,1,4096]{2,1,0:T(1,128)S(1)}, u32[]{:S(2)}, u32[]{:S(2)}) async-start(f32[4,1,4096]{2,1,0:T(1,128)} %reshape.69), calls=%async_computation.1 | async-start | bytes 131072 | tf_op jit(solution)/shard_map/all_to_all | solution.py:30
  20.4 0.0 copy-done.1
  20.4 0.1 add_rsqrt_fusion
  20.5 5.6 %all-to-all-done.1 = f32[4,1,4096]{2,1,0:T(1,128)S(1)} async-done(((f32[4,1,4096]{2,1,0:T(1,128)}), f32[4,1,4096]{2,1,0:T(1,128)S(1)}, u32[]{:S(2)}, u32[]{:S(2)}) %all-to-all-start.1) | async-done | bytes 65568 | tf_op jit(solution)/shard_map/all_to_all | solution.py:30
  26.2 0.9 %reduce.1 = f32[4,4096]{1,0:T(4,128)S(1)} reduce(f32[4,1,4096]{2,1,0:T(1,128)S(1)} %all-to-all-done.1, f32[]{:T(128)} %broadcast.193), dimensions={1}, to_apply=%all_to_all.56.reduce_sub_computation | reduce | bytes 131076 | tf_op jit(solution)/shard_map/all_to_all | solution.py:30
  27.0 0.2 reshape.70
  27.2 0.3 copy.32
  27.6 0.3 all_to_all.59
  27.8 0.5 convolution_multiply_fusion
  28.3 0.4 fusion.8
  28.8 0.3 copy.19
  29.1 0.2 reshape.71
  29.3 8.1 %all_to_all.72 = f32[4,1,4096]{2,1,0:T(1,128)S(1)} all-to-all(f32[4,1,4096]{2,1,0:T(1,128)S(1)} %reshape.71), channel_id=1, replica_groups=mesh['unit'=2,'row'=4,'col'=4] {'col'}, dimensions={0} | all-to-all | bytes 131072 | tf_op jit(solution)/shard_map/all_to_all | solution.py:35
  37.4 0.9 %reduce.2 = f32[4,4096]{1,0:T(4,128)S(1)} reduce(f32[4,1,4096]{2,1,0:T(1,128)S(1)} %all_to_all.72, f32[]{:T(128)} %broadcast.193), dimensions={1}, to_apply=%all_to_all.60.reduce_sub_computation | reduce | bytes 131076 | tf_op jit(solution)/shard_map/all_to_all | solution.py:35
  38.3 0.2 reshape.72
  38.5 0.3 copy.31
  38.8 0.3 all_to_all.63
  39.1 0.5 convolution_bitcast_fusion.1
  39.5 0.3 copy.21
  39.8 0.2 reshape.73
  40.1 6.5 %all_to_all.73 = f32[4,1,4096]{2,1,0:T(1,128)S(1)} all-to-all(f32[4,1,4096]{2,1,0:T(1,128)S(1)} %reshape.73), channel_id=1, replica_groups=mesh['unit'=2,'row'=4,'col'=4] {'row'}, dimensions={0} | all-to-all | bytes 131072 | tf_op jit(solution)/shard_map/all_to_all | solution.py:37
  46.5 0.9 %reduce.3 = f32[4,4096]{1,0:T(4,128)S(1)} reduce(f32[4,1,4096]{2,1,0:T(1,128)S(1)} %all_to_all.73, f32[]{:T(128)} %broadcast.193), dimensions={1}, to_apply=%all_to_all.64.reduce_sub_computation | reduce | bytes 131076 | tf_op jit(solution)/shard_map/all_to_all | solution.py:37
  47.4 0.2 reshape.74
  47.6 0.2 copy.22
  47.8 1.8 %convolution_bitcast_fusion = f32[2,32,16,16]{1,3,2,0:T(8,128)} fusion(f32[2,32,16,16]{3,2,1,0:T(8,128)S(1)} %bitcast.64, s32[32]{0:T(128)S(1)} %multiply_add_fusion.1), kind=kOutput, calls=%fused_computation | convolution fusion | flops 6306816 | bytes 131200 | tf_op jit(solution)/shard_map/dot_general | solution.py:18
  (2 shorter events, 0.0 us)
Async XLA Ops:
  0.0 1.0 %copy-start = (f32[2,32,16,16]{1,3,2,0:T(8,128)S(1)}, f32[2,32,16,16]{1,3,2,0:T(8,128)}, u32[]{:S(2)}) copy-start(f32[2,32,16,16]{1,3,2,0:T(8,128)} %param.4) | copy-start | bytes 196612
  2.8 8.4 %all-to-all-start = ((f32[4,1,4096]{2,1,0:T(1,128)}), f32[4,1,4096]{2,1,0:T(1,128)S(1)}, u32[]{:S(2)}, u32[]{:S(2)}) async-start(f32[4,1,4096]{2,1,0:T(1,128)} %reshape.67), calls=%async_computation | async-start | bytes 131072 | tf_op jit(solution)/shard_map/all_to_all | solution.py:28
  7.0 0.7 %copy-start.2 = (f32[64]{0:T(128)S(1)}, f32[64]{0:T(128)}, u32[]{:S(2)}) copy-start(f32[64]{0:T(128)} %param.6) | copy-start | bytes 772
  7.8 0.7 %copy-start.3 = (f32[32]{0:T(128)S(1)}, f32[32]{0:T(128)}, u32[]{:S(2)}) copy-start(f32[32]{0:T(128)} %param.5) | copy-start | bytes 388
  14.9 5.5 %copy-start.1 = (f32[64]{0:T(128)S(1)}, f32[64]{0:T(128)}, u32[]{:S(2)}) copy-start(f32[64]{0:T(128)} %param.7) | copy-start | bytes 772
  14.9 11.2 %all-to-all-start.1 = ((f32[4,1,4096]{2,1,0:T(1,128)}), f32[4,1,4096]{2,1,0:T(1,128)S(1)}, u32[]{:S(2)}, u32[]{:S(2)}) async-start(f32[4,1,4096]{2,1,0:T(1,128)} %reshape.69), calls=%async_computation.1 | async-start | bytes 131072 | tf_op jit(solution)/shard_map/all_to_all | solution.py:30
where the time goes:
time: 50.1 us; the launch traced here: 49.6 us
  blocking collectives  14.6 us (29%)
  starting transfers between devices  9.74 us (19%)
  local copies, waits for them, and re-layouts  9.15 us (18%)
  waiting for transfers between devices  8.23 us (16%)
  matrix products  4.09 us (8%)
  other arithmetic  3.59 us (7%)
    all_to_all x1, blocking collectives, backward_part(): lax.all_to_all(part_values, 'col', split_axis=3, concat_axis=2, tiled=True)  8.11 us
    all_to_all x1, blocking collectives, backward_part(): lax.all_to_all(part_values, 'row', split_axis=2, concat_axis=1, tiled=True)  6.49 us
    all_to_all x1, waiting for transfers between devices, forward_part(): lax.all_to_all(part_values, 'col', split_axis=2, concat_axis=3, tiled=True)  5.65 us
    all_to_all x1, starting transfers between devices, forward_part(): lax.all_to_all(part_values, 'col', split_axis=2, concat_axis=3, tiled=True)  5.5 us
    unnamed x16, local copies, waits for them, and re-layouts  5.27 us
    all_to_all x1, starting transfers between devices, forward_part(): lax.all_to_all(part_values, 'row', split_axis=1, concat_axis=2, tiled=True)  4.23 us
    dot_general x5, matrix products, to_modes(): jnp.tensordot(values, mode_table(values.shape[dim]), axes=([dim], [0]), p...  3.59 us
    all_to_all x1, waiting for transfers between devices, forward_part(): lax.all_to_all(part_values, 'row', split_axis=1, concat_axis=2, tiled=True)  2.58 us
  transfers between devices with their start and end apart: 2, of which 2 were waited for; matrix products, arithmetic and copies ran while one was open for 1% of the time, Pallas kernels for 0%

commit v1 on v0

--- a/solution.py
+++ b/solution.py
@@ -2,6 +2,17 @@
 import jax.numpy as jnp
 from jax import lax
 from jax.sharding import PartitionSpec as P
+
+
+def in_blocks(x, dim, devices):
+    before, after = (x.shape[:dim], x.shape[dim + 1 :])
+    return jnp.moveaxis(x.reshape(*before, devices, -1, *after), dim, 0)
+
+
+def in_order(blocks, dim):
+    blocks = jnp.moveaxis(blocks, 0, dim)
+    dims = blocks.shape
+    return blocks.reshape(*dims[:dim], dims[dim] * dims[dim + 1], *dims[dim + 2 :])
 
 
 def mode_table(count):
@@ -27,7 +38,15 @@
         part_values = to_modes(part_values, 1)
         part_values = lax.all_to_all(part_values, "row", split_axis=1, concat_axis=2, tiled=True)
         part_values = to_modes(part_values, 2)
-        part_values = lax.all_to_all(part_values, "col", split_axis=2, concat_axis=3, tiled=True)
+        size, place = (lax.axis_size("col"), lax.axis_index("col"))
+        blocks = in_blocks(part_values, 2, size)
+        whole = blocks
+        for step in range(1, size):
+            target, source = ((place + step) % size, (place - step) % size)
+            sent = lax.dynamic_index_in_dim(blocks, target, 0)
+            other = lax.ppermute(sent, "col", [(i, (i + step) % size) for i in range(size)])
+            whole = lax.dynamic_update_slice_in_dim(whole, other, source, axis=0)
+        part_values = in_order(whole, 3)
         return to_modes(part_values, 3)
 
     def backward_part(part_values):

time: 50.1 us -> 59 us (1.18)
  local copies, waits for them, and re-layouts: 9.15 us -> 17 us
  blocking collectives: 14.6 us -> 18 us
  waiting for transfers between devices: 8.23 us -> 6.21 us
  other arithmetic: 3.59 us -> 2.61 us
  starting transfers between devices: 9.74 us -> 10.4 us
    dynamic_update_slice x0 -> x3, local copies, waits for them, and re-layouts: none -> 8.42 us  [forward_part(): whole = lax.dynamic_update_slice_in_dim(whole, other, source, axis=0)]
    ppermute x0 -> x3, starting transfers between devices: none -> 6.18 us  [forward_part(): lax.ppermute(sent, 'col', [(i, (i + step) % size) for i in range(size)])]
    all_to_all x1 -> x0, waiting for transfers between devices: 5.65 us -> none  [forward_part(): lax.all_to_all(part_values, 'col', split_axis=2, concat_axis=3, tiled=True)]
    all_to_all x1 -> x0, starting transfers between devices: 5.5 us -> none  [forward_part(): lax.all_to_all(part_values, 'col', split_axis=2, concat_axis=3, tiled=True)]
    ppermute x0 -> x3, waiting for transfers between devices: none -> 3.63 us  [forward_part(): lax.ppermute(sent, 'col', [(i, (i + step) % size) for i in range(size)])]
    all_to_all x1, blocking collectives: 8.11 us -> 11.6 us  [backward_part(): lax.all_to_all(part_values, 'col', split_axis=3, concat_axis=2, tiled=True)]
    unnamed x16 -> x14, local copies, waits for them, and re-layouts: 5.27 us -> 4.2 us
    all_to_all x1 -> x0, other arithmetic: 0.86 us -> none  [forward_part(): lax.all_to_all(part_values, 'col', split_axis=2, concat_axis=3, tiled=True)]
  transfers between devices with their start and end apart: 2 -> 4, of which waited for: 2 -> 3; matrix products, arithmetic and copies ran while one was open for 1% -> 11% of each run, Pallas kernels for 0% -> 0%
where the time goes in v1:
time: 59 us; the launch traced here: 58.6 us
  blocking collectives  18 us (31%)
  local copies, waits for them, and re-layouts  17 us (29%)
  starting transfers between devices  10.4 us (18%)
  waiting for transfers between devices  6.21 us (11%)
  matrix products  4.09 us (7%)
  other arithmetic  2.61 us (4%)
    all_to_all x1, blocking collectives, backward_part(): lax.all_to_all(part_values, 'col', split_axis=3, concat_axis=2, tiled=True)  11.6 us
    dynamic_update_slice x3, local copies, waits for them, and re-layouts, forward_part(): whole = lax.dynamic_update_slice_in_dim(whole, other, source, axis=0)  8.42 us
    all_to_all x1, blocking collectives, backward_part(): lax.all_to_all(part_values, 'row', split_axis=2, concat_axis=1, tiled=True)  6.49 us
    ppermute x3, starting transfers between devices, forward_part(): lax.ppermute(sent, 'col', [(i, (i + step) % size) for i in range(size)])  6.18 us
    all_to_all x1, starting transfers between devices, forward_part(): lax.all_to_all(part_values, 'row', split_axis=1, concat_axis=2, tiled=True)  4.23 us
    unnamed x14, local copies, waits for them, and re-layouts  4.2 us
    ppermute x3, waiting for transfers between devices, forward_part(): lax.ppermute(sent, 'col', [(i, (i + step) % size) for i in range(size)])  3.63 us
    dot_general x5, matrix products, to_modes(): jnp.tensordot(values, mode_table(values.shape[dim]), axes=([dim], [0]), p...  3.59 us
  transfers between devices with their start and end apart: 4, of which 3 were waited for; matrix products, arithmetic and copies ran while one was open for 11% of the time, Pallas kernels for 0%

profile of v1, /device:TPU:0, one launch (start us, length us, event | category | flops | bytes accessed | tf_op | source)
XLA Modules:
  0.0 58.6 jit_solution(1823772524335928814)
XLA Ops:
  0.0 0.9 %copy-done = f32[2,32,16,16]{1,3,2,0:T(8,128)S(1)} copy-done((f32[2,32,16,16]{1,3,2,0:T(8,128)S(1)}, f32[2,32,16,16]{1,3,2,0:T(8,128)}, u32[]{:S(2)}) %copy-start) | copy-done | bytes 65560
  1.0 0.5 fusion.47
  1.5 0.5 copy.17
  1.9 0.9 %reshape.78 = f32[4,1,4096]{2,1,0:T(1,128)} reshape(f32[32,2,16,16]{3,2,1,0:T(8,128)S(1)} %bitcast.65) | data formatting | bytes 131072
  2.8 4.2 %all-to-all-start = ((f32[4,1,4096]{2,1,0:T(1,128)}), f32[4,1,4096]{2,1,0:T(1,128)S(1)}, u32[]{:S(2)}, u32[]{:S(2)}) async-start(f32[4,1,4096]{2,1,0:T(1,128)} %reshape.78), calls=%async_computation | async-start | bytes 131072 | tf_op jit(solution)/shard_map/all_to_all | solution.py:39
  7.0 0.7 %copy-done.2 = f32[64]{0:T(128)S(1)} copy-done((f32[64]{0:T(128)S(1)}, f32[64]{0:T(128)}, u32[]{:S(2)}) %copy-start.2) | copy-done | bytes 280
  7.7 0.1 dynamic_slice.20
  7.8 0.7 %copy-done.3 = f32[32]{0:T(128)S(1)} copy-done((f32[32]{0:T(128)S(1)}, f32[32]{0:T(128)}, u32[]{:S(2)}) %copy-start.3) | copy-done | bytes 152
  8.6 2.6 %all-to-all-done = f32[4,1,4096]{2,1,0:T(1,128)S(1)} async-done(((f32[4,1,4096]{2,1,0:T(1,128)}), f32[4,1,4096]{2,1,0:T(1,128)S(1)}, u32[]{:S(2)}, u32[]{:S(2)}) %all-to-all-start) | async-done | bytes 65568 | tf_op jit(solution)/shard_map/all_to_all | solution.py:39
  11.2 0.5 broadcast.199
  11.7 0.8 %reduce = f32[4,4096]{1,0:T(4,128)S(1)} reduce(f32[4,1,4096]{2,1,0:T(1,128)S(1)} %all-to-all-done, f32[]{:T(128)} %broadcast.199), dimensions={1}, to_apply=%all_to_all.39.reduce_sub_computation | reduce | bytes 131076 | tf_op jit(solution)/shard_map/all_to_all | solution.py:39
  12.5 0.2 reshape.79
  12.7 0.2 copy.19
  12.9 0.3 all_to_all.42
  13.2 0.5 convolution_bitcast_fusion.2
  13.7 0.3 reshape.72
  13.9 0.4 constant_dynamic-slice_fusion
  14.3 0.1 copy.21
  14.4 2.1 %collective-permute-start = (f32[1,2,8,16,16]{4,0,3,2,1:T(1,128)S(1)}, f32[1,2,8,16,16]{4,0,3,2,1:T(1,128)S(1)}, u32[]{:S(2)}, u32[]{:S(2)}) collective-permute-start(f32[1,2,8,16,16]{4,0,3,2,1:T(1,128)S(1)} %bitcast.74), channel_id=1, source_target_pairs={{0,1},{1,2},{2,3},{3,0},{4,5},{5,6},{6,7},{7,4},{8,9},{9,10},{10,1... | collective-permute-start | bytes 49160 | tf_op jit(solution)/shard_map/ppermute | solution.py:47
  16.6 0.1 copy.22
  16.6 2.7 %collective-permute-start.1 = (f32[1,2,8,16,16]{4,0,3,2,1:T(1,128)S(1)}, f32[1,2,8,16,16]{4,0,3,2,1:T(1,128)S(1)}, u32[]{:S(2)}, u32[]{:S(2)}) collective-permute-start(f32[1,2,8,16,16]{4,0,3,2,1:T(1,128)S(1)} %bitcast.73), channel_id=1, source_target_pairs={{0,2},{1,3},{2,0},{3,1},{4,6},{5,7},{6,4},{7,5},{8,10},{9,11},{10,... | collective-permute-start | bytes 49160 | tf_op jit(solution)/shard_map/ppermute | solution.py:47
  19.3 0.1 copy.23
  19.4 1.4 %collective-permute-start.2 = (f32[1,2,8,16,16]{4,0,3,2,1:T(1,128)S(1)}, f32[1,2,8,16,16]{4,0,3,2,1:T(1,128)S(1)}, u32[]{:S(2)}, u32[]{:S(2)}) collective-permute-start(f32[1,2,8,16,16]{4,0,3,2,1:T(1,128)S(1)} %bitcast.72), channel_id=1, source_target_pairs={{0,3},{1,0},{2,1},{3,2},{4,7},{5,4},{6,5},{7,6},{8,11},{9,8},{10,9... | collective-permute-start | bytes 49160 | tf_op jit(solution)/shard_map/ppermute | solution.py:47
  20.8 0.1 add_rsqrt_fusion
  21.0 0.2 copy.20
  21.2 1.8 %collective-permute-done = f32[1,2,8,16,16]{4,0,3,2,1:T(1,128)S(1)} collective-permute-done((f32[1,2,8,16,16]{4,0,3,2,1:T(1,128)S(1)}, f32[1,2,8,16,16]{4,0,3,2,1:T(1,128)S(1)}, u32[]{:S(2)}, u32[]{:S(2)}) %collective-permute-start) | collective-permute-done | bytes 16416 | tf_op jit(solution)/shard_map/ppermute | solution.py:47
  23.0 2.8 %dynamic_update_slice.9 = f32[4,2,8,16,16]{4,0,3,2,1:T(4,128)S(1)} dynamic-update-slice(f32[4,2,8,16,16]{4,0,3,2,1:T(4,128)S(1)} %bitcast.63, f32[1,2,8,16,16]{4,0,3,2,1:T(1,128)S(1)} %collective-permute-done, s32[]{:T(128)S(6)} %select_n.85, s32[]{:T(128)} %constant.104.clone.1, s32[]{:T(128)} %constant.104.clone.1, s32[]{:T(128)} %constant.104.clone.1, s32[]{:T(128)} %constant.104.clone.1) | dynamic-update-slice | bytes 32772 | tf_op jit(solution)/shard_map/dynamic_update_slice | solution.py:48
  25.8 1.8 %collective-permute-done.1 = f32[1,2,8,16,16]{4,0,3,2,1:T(1,128)S(1)} collective-permute-done((f32[1,2,8,16,16]{4,0,3,2,1:T(1,128)S(1)}, f32[1,2,8,16,16]{4,0,3,2,1:T(1,128)S(1)}, u32[]{:S(2)}, u32[]{:S(2)}) %collective-permute-start.1) | collective-permute-done | bytes 16416 | tf_op jit(solution)/shard_map/ppermute | solution.py:47
  27.6 2.8 %dynamic_update_slice.10 = f32[4,2,8,16,16]{4,0,3,2,1:T(4,128)S(1)} dynamic-update-slice(f32[4,2,8,16,16]{4,0,3,2,1:T(4,128)S(1)} %dynamic_update_slice.9, f32[1,2,8,16,16]{4,0,3,2,1:T(1,128)S(1)} %collective-permute-done.1, s32[]{:T(128)S(6)} %select_n.89, s32[]{:T(128)} %constant.104.clone.1, s32[]{:T(128)} %constant.104.clone.1, s32[]{:T(128)} %constant.104.clone.1, s32[]{:T(128)} %constant.104.clone.1) | dynamic-update-slice | bytes 32772 | tf_op jit(solution)/shard_map/dynamic_update_slice | solution.py:48
  30.5 2.8 %dynamic_update_slice.11 = f32[4,2,8,16,16]{4,0,3,2,1:T(4,128)S(1)} dynamic-update-slice(f32[4,2,8,16,16]{4,0,3,2,1:T(4,128)S(1)} %dynamic_update_slice.10, f32[1,2,8,16,16]{4,0,3,2,1:T(1,128)S(1)} %collective-permute-done.2, s32[]{:T(128)S(6)} %select_n.93, s32[]{:T(128)} %constant.104.clone.1, s32[]{:T(128)} %constant.104.clone.1, s32[]{:T(128)} %constant.104.clone.1, s32[]{:T(128)} %constant.104.clone.1) | dynamic-update-slice | bytes 32772 | tf_op jit(solution)/shard_map/dynamic_update_slice | solution.py:48
  33.3 0.3 reshape.73
  33.5 0.4 convolution_multiply_fusion
  34.0 0.5 fusion.8
  34.5 0.3 copy.24
  34.7 0.2 reshape.80
  35.0 11.6 %all_to_all.54 = f32[4,1,4096]{2,1,0:T(1,128)S(1)} all-to-all(f32[4,1,4096]{2,1,0:T(1,128)S(1)} %reshape.80), channel_id=1, replica_groups=mesh['unit'=2,'row'=4,'col'=4] {'col'}, dimensions={0} | all-to-all | bytes 131072 | tf_op jit(solution)/shard_map/all_to_all | solution.py:54
  46.5 0.8 %reduce.1 = f32[4,4096]{1,0:T(4,128)S(1)} reduce(f32[4,1,4096]{2,1,0:T(1,128)S(1)} %all_to_all.54, f32[]{:T(128)} %broadcast.199), dimensions={1}, to_apply=%all_to_all.43.reduce_sub_computation | reduce | bytes 131076 | tf_op jit(solution)/shard_map/all_to_all | solution.py:54
  47.4 0.2 reshape.81
  47.6 0.3 copy.35
  47.9 0.3 all_to_all.46
  48.2 0.5 convolution_bitcast_fusion.1
  48.6 0.3 copy.26
  48.9 0.2 reshape.82
  49.2 6.5 %all_to_all.55 = f32[4,1,4096]{2,1,0:T(1,128)S(1)} all-to-all(f32[4,1,4096]{2,1,0:T(1,128)S(1)} %reshape.82), channel_id=1, replica_groups=mesh['unit'=2,'row'=4,'col'=4] {'row'}, dimensions={0} | all-to-all | bytes 131072 | tf_op jit(solution)/shard_map/all_to_all | solution.py:56
  55.6 0.8 %reduce.2 = f32[4,4096]{1,0:T(4,128)S(1)} reduce(f32[4,1,4096]{2,1,0:T(1,128)S(1)} %all_to_all.55, f32[]{:T(128)} %broadcast.199), dimensions={1}, to_apply=%all_to_all.47.reduce_sub_computation | reduce | bytes 131076 | tf_op jit(solution)/shard_map/all_to_all | solution.py:56
  56.5 0.2 reshape.83
  56.7 0.2 copy.27
  56.8 1.8 %convolution_bitcast_fusion = f32[2,32,16,16]{1,3,2,0:T(8,128)} fusion(f32[2,32,16,16]{3,2,1,0:T(8,128)S(1)} %bitcast.67, s32[32]{0:T(128)S(1)} %multiply_add_fusion.1), kind=kOutput, calls=%fused_computation | convolution fusion | flops 6306816 | bytes 131200 | tf_op jit(solution)/shard_map/dot_general | solution.py:29
  (10 shorter events, 0.2 us)
Async XLA Ops:
  0.0 1.0 %copy-start = (f32[2,32,16,16]{1,3,2,0:T(8,128)S(1)}, f32[2,32,16,16]{1,3,2,0:T(8,128)}, u32[]{:S(2)}) copy-start(f32[2,32,16,16]{1,3,2,0:T(8,128)} %param.4) | copy-start | bytes 196612
  2.8 8.4 %all-to-all-start = ((f32[4,1,4096]{2,1,0:T(1,128)}), f32[4,1,4096]{2,1,0:T(1,128)S(1)}, u32[]{:S(2)}, u32[]{:S(2)}) async-start(f32[4,1,4096]{2,1,0:T(1,128)} %reshape.78), calls=%async_computation | async-start | bytes 131072 | tf_op jit(solution)/shard_map/all_to_all | solution.py:39
  7.0 0.7 %copy-start.2 = (f32[64]{0:T(128)S(1)}, f32[64]{0:T(128)}, u32[]{:S(2)}) copy-start(f32[64]{0:T(128)} %param.6) | copy-start | bytes 772
  7.8 0.7 %copy-start.3 = (f32[32]{0:T(128)S(1)}, f32[32]{0:T(128)}, u32[]{:S(2)}) copy-start(f32[32]{0:T(128)} %param.5) | copy-start | bytes 388
  14.4 8.6 %collective-permute-start = (f32[1,2,8,16,16]{4,0,3,2,1:T(1,128)S(1)}, f32[1,2,8,16,16]{4,0,3,2,1:T(1,128)S(1)}, u32[]{:S(2)}, u32[]{:S(2)}) collective-permute-start(f32[1,2,8,16,16]{4,0,3,2,1:T(1,128)S(1)} %bitcast.74), channel_id=1, source_target_pairs={{0,1},{1,2},{2,3},{3,0},{4,5},{5,6},{6,7},{7,4},{8,9},{9,10},{10,1... | collective-permute-start | bytes 49160 | tf_op jit(solution)/shard_map/ppermute | solution.py:47
  16.6 11.0 %collective-permute-start.1 = (f32[1,2,8,16,16]{4,0,3,2,1:T(1,128)S(1)}, f32[1,2,8,16,16]{4,0,3,2,1:T(1,128)S(1)}, u32[]{:S(2)}, u32[]{:S(2)}) collective-permute-start(f32[1,2,8,16,16]{4,0,3,2,1:T(1,128)S(1)} %bitcast.73), channel_id=1, source_target_pairs={{0,2},{1,3},{2,0},{3,1},{4,6},{5,7},{6,4},{7,5},{8,10},{9,11},{10,... | collective-permute-start | bytes 49160 | tf_op jit(solution)/shard_map/ppermute | solution.py:47
  19.4 1.4 %copy-start.1 = (f32[64]{0:T(128)S(1)}, f32[64]{0:T(128)}, u32[]{:S(2)}) copy-start(f32[64]{0:T(128)} %param.7) | copy-start | bytes 772
  19.4 11.0 %collective-permute-start.2 = (f32[1,2,8,16,16]{4,0,3,2,1:T(1,128)S(1)}, f32[1,2,8,16,16]{4,0,3,2,1:T(1,128)S(1)}, u32[]{:S(2)}, u32[]{:S(2)}) collective-permute-start(f32[1,2,8,16,16]{4,0,3,2,1:T(1,128)S(1)} %bitcast.72), channel_id=1, source_target_pairs={{0,3},{1,0},{2,1},{3,2},{4,7},{5,4},{6,5},{7,6},{8,11},{9,8},{10,9... | collective-permute-start | bytes 49160 | tf_op jit(solution)/shard_map/ppermute | solution.py:47
